TPU v7x, 32 devices: a whole 2x2x4 slice. The times are simulated.
32 devices in a mesh: group: 2 (over y), expert: 4 (over x, core), tensor: 4 (over z).
Axes of the slice: x: 2, y: 2, z: 4, core: 2. Of those that a mesh axis runs over, the one named last changes fastest.
Arguments:
- tokens: bfloat16 [512, 4096], P(('group', 'expert'), 'tensor'), parts along dimension 0, may hold values from -6 to 6
- w_gate: bfloat16 [8, 4096, 1536], P('expert', 'tensor'), may hold values from -0.125 to 0.125
- w_up: bfloat16 [8, 4096, 1536], P('expert', 'tensor'), may hold values from -0.125 to 0.125
- w_down: bfloat16 [8, 1536, 4096], P('expert', None, 'tensor'), may hold values from -0.15625 to 0.15625
- expert_ids: int32 [512, 8], P(('group', 'expert')), parts along dimension 0, may hold values from 0 to 7, as said below
- route_weights: float32 [512, 8], P(('group', 'expert')), parts along dimension 0, may hold values from 0.05 to 0.5
Outputs:
- mixed_out: bfloat16 [512, 4096], P(('group', 'expert'), 'tensor'), parts along dimension 0
There are 2 independent parts, one for each index of `group`. A program takes and returns all parts, laid end to end along the dimension named above; an argument that names none is the same for every part. Nothing has to cross between parts.
Inputs may be any that keep to these rules, and one draw needn't show every extreme that they name: `expert_ids`: each row names 8 different experts. In each aligned block of 64 rows no expert is named by more than 64 rows, and one expert, the same in every block of a part, is named by exactly 64 rows of every block.
All inputs are finite; a program needn't handle non-finite values.
Results may differ from a plain program's by a relative error of at most 0.0057.
Values may be sent and summed in bfloat16 or wider, within the bound.
A program may use at most 128 MiB of HBM per device.

v0:
```python
import jax
import jax.numpy as jnp
from jax import lax
from jax.sharding import PartitionSpec as P


def slot_numbers(flat_ids, experts_all):
    labels = jnp.arange(experts_all, dtype=jnp.int32)
    onehot = (flat_ids[:, None] == labels[None, :]).astype(jnp.int32)
    before = jnp.cumsum(onehot, axis=0) - onehot
    return jnp.sum(before * onehot, axis=1)


def per_device(tokens, w_gate, w_up, w_down, expert_ids, route_weights):
    n_expert = lax.axis_size("expert")
    held_experts = w_gate.shape[0]
    experts_all = held_experts * n_expert
    tok_rows = tokens.shape[0]
    col_share = tokens.shape[1]
    per_token = expert_ids.shape[1]
    capacity = min(tok_rows, 2 * tok_rows * per_token // experts_all)
    flat_ids = expert_ids.reshape(tok_rows * per_token)
    position = flat_ids * capacity + slot_numbers(flat_ids, experts_all)
    owners = jnp.arange(tok_rows * per_token, dtype=jnp.int32) // per_token
    source = jnp.full((experts_all * capacity,), -1, jnp.int32).at[position].set(owners)
    filled = (source >= 0)[:, None]
    picked_rows = jnp.where(filled, tokens[jnp.maximum(source, 0)], jnp.zeros((), tokens.dtype))
    outgoing = picked_rows.reshape(n_expert, held_experts, capacity, col_share)
    received = lax.all_to_all(outgoing, "expert", split_axis=0, concat_axis=0, tiled=True)
    gate_part = jnp.einsum("sjnd,jdf->sjnf", received, w_gate, preferred_element_type=jnp.float32)
    up_part = jnp.einsum("sjnd,jdf->sjnf", received, w_up, preferred_element_type=jnp.float32)
    gate_share = lax.psum_scatter(gate_part, "tensor", scatter_dimension=3, tiled=True)
    up_share = lax.psum_scatter(up_part, "tensor", scatter_dimension=3, tiled=True)
    hidden_share = (jax.nn.silu(gate_share) * up_share).astype(jnp.bfloat16)
    hidden = lax.all_gather(hidden_share, "tensor", axis=3, tiled=True)
    result = jnp.einsum("sjnf,jfd->sjnd", hidden, w_down, preferred_element_type=jnp.float32)
    returned = result.astype(jnp.bfloat16)
    combined = lax.all_to_all(returned, "expert", split_axis=0, concat_axis=0, tiled=True).reshape(
        experts_all * capacity, col_share
    )
    picked = combined[position].reshape(tok_rows, per_token, col_share).astype(jnp.float32)
    mixed_out = jnp.sum(picked * route_weights[:, :, None], axis=1)
    return mixed_out.astype(jnp.bfloat16)


def solution(mesh):
    in_specs = (
        P(("group", "expert"), "tensor"),
        P("expert", "tensor", None),
        P("expert", "tensor", None),
        P("expert", None, "tensor"),
        P(("group", "expert"), None),
        P(("group", "expert"), None),
    )
    out_specs = P(("group", "expert"), "tensor")
    return jax.shard_map(
        per_device, mesh=mesh, in_specs=in_specs, out_specs=out_specs, check_vma=False
    )
```

profile of v0, /device:TPU:0, one launch (start us, length us, event | category | flops | bytes accessed | tf_op | source)
XLA Modules:
  0.0 236.0 jit_solution(6427868677075579159)
XLA Ops:
  6.5 0.0 copy-start
  6.5 0.0 reduce-scatter.3.cloned.1.call-start
  6.5 0.8 copy.16
  7.3 0.1 eq.29
  7.4 0.1 eq.25
  7.5 0.7 broadcast_multiply_fusion
  8.2 1.1 reduce-window.6
  9.4 0.2 slice_reduce_fusion
  9.6 0.1 copy.15
  9.7 0.1 mul.32
  9.8 0.1 fusion.22
  9.9 2.4 %scatter_custom_fusion = s32[512]{0:T(512)S(1)} fusion(s32[512]{0:T(512)S(1)} %bitcast.47, s32[512]{0:T(512)S(1)} %add_select_fusion, s32[]{:T(128)} %constant.27.clone.1), kind=kCustom, calls=%fused_computation.39 | custom fusion | bytes 2052 | tf_op jit(solution)/shard_map/scatter | solution.py:25
  12.4 0.1 broadcast_in_dim.26
  12.5 0.0 copy-done
  12.5 2.1 gather_fusion
  14.5 0.1 broadcast_select_fusion
  14.7 18.5 %all_to_all.10 = bf16[4,2,64,1024]{3,2,1,0:T(8,128)(2,1)S(1)} all-to-all(bf16[4,2,64,1024]{3,2,1,0:T(8,128)(2,1)S(1)} %broadcast_select_fusion), channel_id=1, replica_groups=mesh['group'=2,'expert'=4,'tensor'=4] {'expert'}, dimensions={0} | all-to-all | bytes 2097152 | tf_op jit(solution)/shard_map/all_to_all | solution.py:29
  33.2 6.3 %fusion.6 = f32[4,2,64,1536]{3,2,0,1:T(8,128)} fusion(bf16[2,1024,1536]{2,1,0:T(8,128)(2,1)} %param.7, bf16[4,2,64,1024]{3,2,1,0:T(8,128)(2,1)S(1)} %all_to_all.10), kind=kOutput, calls=%fused_computation.9 | convolution fusion | flops 1610612736 | bytes 10485760 | tf_op jit(solution)/shard_map/sjnd,jdf->sjnf/dot_general | solution.py:30
  39.4 0.0 reduce-scatter.3.cloned.1.call-update
  39.5 0.0 reduce-scatter.5.cloned.1.call-start
  39.5 6.3 %fusion.9 = f32[4,2,64,1536]{3,2,0,1:T(8,128)} fusion(bf16[2,1024,1536]{2,1,0:T(8,128)(2,1)} %param.8, bf16[4,2,64,1024]{3,2,1,0:T(8,128)(2,1)S(1)} %all_to_all.10), kind=kOutput, calls=%fused_computation.10 | convolution fusion | flops 1610612736 | bytes 10485760 | tf_op jit(solution)/shard_map/sjnd,jdf->sjnf/dot_general | solution.py:31
  45.8 0.0 reduce-scatter.5.cloned.1.call-update
  45.8 0.0 all-gather.2.cloned.1.call-start
  45.9 54.4 %reduce-scatter.3.cloned.1.call-done = f32[4,2,64,384]{3,2,0,1:T(8,128)} async-done(((f32[4,2,64,1536]{3,2,0,1:T(8,128)}), f32[4,2,64,384]{3,2,0,1:T(8,128)}) %reduce-scatter.3.cloned.1.call-update) | async-done | bytes 786448 | tf_op jit(solution)/shard_map/reduce_scatter | solution.py:32
  100.3 62.6 %reduce-scatter.5.cloned.1.call-done = f32[4,2,64,384]{3,2,0,1:T(8,128)} async-done(((f32[4,2,64,1536]{3,2,0,1:T(8,128)}), f32[4,2,64,384]{3,2,0,1:T(8,128)}) %reduce-scatter.5.cloned.1.call-update) | async-done | bytes 786448 | tf_op jit(solution)/shard_map/reduce_scatter | solution.py:33
  163.0 2.3 multiply_convert_fusion
  165.3 0.0 all-gather.2.cloned.1.call-update
  165.3 0.0 copy-start.1
  165.3 36.7 %all-gather.2.cloned.1.call-done = bf16[4,2,64,1536]{3,2,0,1:T(8,128)(2,1)} async-done(((bf16[4,2,64,384]{3,2,0,1:T(8,128)(2,1)}), bf16[4,2,64,1536]{3,2,0,1:T(8,128)(2,1)}) %all-gather.2.cloned.1.call-update) | async-done | bytes 1572880 | tf_op jit(solution)/shard_map/all_gather | solution.py:35
  202.0 5.1 %fusion.16 = bf16[4,2,64,1024]{3,2,0,1:T(8,128)(2,1)S(1)} fusion(bf16[4,2,64,1536]{3,2,0,1:T(8,128)(2,1)} %all-gather.2.cloned.1.call-done, bf16[2,1536,1024]{2,1,0:T(8,128)(2,1)} %param.9), kind=kOutput, calls=%fused_computation.14 | convolution fusion | flops 1611137024 | bytes 8912896 | tf_op jit(solution)/shard_map/sjnf,jfd->sjnd/dot_general | solution.py:36
  207.1 1.1 copy.20
  208.1 3.5 %all-to-all-start.1 = ((bf16[4,2,64,1024]{3,2,1,0:T(8,128)(2,1)}), bf16[4,2,64,1024]{3,2,1,0:T(8,128)(2,1)S(1)}, u32[]{:S(2)}, u32[]{:S(2)}) async-start(bf16[4,2,64,1024]{3,2,1,0:T(8,128)(2,1)} %copy.20), calls=%async_computation.3 | async-start | bytes 2097152 | tf_op jit(solution)/shard_map/all_to_all | solution.py:38
  211.7 0.0 copy-done.1
  211.7 0.1 copy.21
  211.8 14.3 %all-to-all-done.1 = bf16[4,2,64,1024]{3,2,1,0:T(8,128)(2,1)S(1)} async-done(((bf16[4,2,64,1024]{3,2,1,0:T(8,128)(2,1)}), bf16[4,2,64,1024]{3,2,1,0:T(8,128)(2,1)S(1)}, u32[]{:S(2)}, u32[]{:S(2)}) %all-to-all-start.1) | async-done | bytes 1048608 | tf_op jit(solution)/shard_map/all_to_all | solution.py:38
  226.1 2.0 gather_fusion.1
  228.1 1.4 fusion.12
  (9 shorter events, 0.1 us)
Async XLA Ops:
  6.5 6.0 %copy-start = (bf16[64,1024]{1,0:T(8,128)(2,1)S(1)}, bf16[64,1024]{1,0:T(8,128)(2,1)}, u32[]{:S(2)}) copy-start(bf16[64,1024]{1,0:T(8,128)(2,1)} %param.6) | copy-start | bytes 393220
  6.5 93.8 %reduce-scatter.3.cloned.1.call-start = ((), (), s32[]{:S(2)}) async-start(), calls=%async_computation.4 | async-start | bytes 3932160 | tf_op jit(solution)/shard_map/reduce_scatter | solution.py:32
  39.5 123.5 %reduce-scatter.5.cloned.1.call-start = ((), (), s32[]{:S(2)}) async-start(), calls=%async_computation.5 | async-start | bytes 3932160 | tf_op jit(solution)/shard_map/reduce_scatter | solution.py:33
  45.8 156.2 %all-gather.2.cloned.1.call-start = ((), (), s32[]{:S(2)}) async-start(), calls=%async_computation.6 | async-start | bytes 1966080 | tf_op jit(solution)/shard_map/all_gather | solution.py:35
  165.3 46.3 %copy-start.1 = (f32[64,8]{0,1:T(8,128)S(1)}, f32[64,8]{0,1:T(8,128)}, u32[]{:S(2)}) copy-start(f32[64,8]{0,1:T(8,128)} %param.11) | copy-start | bytes 6148
  208.1 17.9 %all-to-all-start.1 = ((bf16[4,2,64,1024]{3,2,1,0:T(8,128)(2,1)}), bf16[4,2,64,1024]{3,2,1,0:T(8,128)(2,1)S(1)}, u32[]{:S(2)}, u32[]{:S(2)}) async-start(bf16[4,2,64,1024]{3,2,1,0:T(8,128)(2,1)} %copy.20), calls=%async_computation.3 | async-start | bytes 2097152 | tf_op jit(solution)/shard_map/all_to_all | solution.py:38
Sparse Core Ops, SparseCore 0:
  39.6 60.6 reduce-scatter.2
  102.6 60.3 reduce-scatter.4
  165.4 36.5 all-gather.1
where the time goes:
time: 236 us
  waiting for transfers between devices  168 us (71%)
  blocking collectives  18.5 us (8%)
  matrix products  17.6 us (7%)
  between operations  13.2 us (6%)
  local copies, waits for them, and re-layouts  9.18 us (4%)
  other arithmetic  5.83 us (2%)
  starting transfers between devices  3.6 us (2%)
    reduce_scatter x1, waiting for transfers between devices, per_device(): lax.psum_scatter(up_part, 'tensor', scatter_dimension=3, tiled=True)  62.6 us
    reduce_scatter x1, waiting for transfers between devices, per_device(): lax.psum_scatter(gate_part, 'tensor', scatter_dimension=3, tiled=True)  54.4 us
    all_gather x1, waiting for transfers between devices, per_device(): hidden = lax.all_gather(hidden_share, 'tensor', axis=3, tiled=True)  36.7 us
    all_to_all x1, blocking collectives, per_device(): lax.all_to_all(outgoing, 'expert', split_axis=0, concat_axis=0, tiled=True)  18.5 us
    all_to_all x1, waiting for transfers between devices, per_device(): lax.all_to_all(returned, 'expert', split_axis=0, concat_axis=0, tiled=True)  14.3 us
    dot_general x1, matrix products, per_device(): jnp.einsum('sjnd,jdf->sjnf', received, w_up, preferred_element_type=jnp.f...  6.3 us
    dot_general x1, matrix products, per_device(): jnp.einsum('sjnd,jdf->sjnf', received, w_gate, preferred_element_type=jnp...  6.27 us
    dot_general x1, matrix products, per_device(): jnp.einsum('sjnf,jfd->sjnd', hidden, w_down, preferred_element_type=jnp.f...  5.06 us
  transfers between devices with their start and end apart: 4, of which 4 were waited for; matrix products, arithmetic and copies ran while one was open for 3% of the time, Pallas kernels for 0%

commit v1 on v0

--- a/solution.py
+++ b/solution.py
@@ -2,6 +2,18 @@
 import jax.numpy as jnp
 from jax import lax
 from jax.sharding import PartitionSpec as P
+
+
+def ring_product(x, axis, dim, term):
+    count, index = (lax.axis_size(axis), lax.axis_index(axis))
+    left = [(i, (i - 1) % count) for i in range(count)]
+    width = x.shape[dim]
+    held = x
+    running = term(held, index * width)
+    for turn in range(1, count):
+        held = lax.ppermute(held, axis, left)
+        running = running + term(held, (index + turn) % count * width)
+    return running
 
 
 def slot_numbers(flat_ids, experts_all):
@@ -32,8 +44,17 @@
     gate_share = lax.psum_scatter(gate_part, "tensor", scatter_dimension=3, tiled=True)
     up_share = lax.psum_scatter(up_part, "tensor", scatter_dimension=3, tiled=True)
     hidden_share = (jax.nn.silu(gate_share) * up_share).astype(jnp.bfloat16)
-    hidden = lax.all_gather(hidden_share, "tensor", axis=3, tiled=True)
-    result = jnp.einsum("sjnf,jfd->sjnd", hidden, w_down, preferred_element_type=jnp.float32)
+    result = ring_product(
+        hidden_share,
+        "tensor",
+        3,
+        lambda part, start: jnp.einsum(
+            "sjnf,jfd->sjnd",
+            part,
+            lax.dynamic_slice_in_dim(w_down, start, part.shape[3], axis=1),
+            preferred_element_type=jnp.float32,
+        ),
+    )
     returned = result.astype(jnp.bfloat16)
     combined = lax.all_to_all(returned, "expert", split_axis=0, concat_axis=0, tiled=True).reshape(
         experts_all * capacity, col_share

time: 236 us -> 229 us (0.970)
  waiting for transfers between devices: 168 us -> 149 us
  starting transfers between devices: 3.6 us -> 14.1 us
    all_gather x1 -> x0, waiting for transfers between devices: 36.7 us -> none  [per_device(): hidden = lax.all_gather(hidden_share, 'tensor', axis=3, tiled=True)]
    ppermute x0 -> x3, waiting for transfers between devices: none -> 17.8 us  [ring_product(): held = lax.ppermute(held, axis, left)]
    ppermute x0 -> x3, starting transfers between devices: none -> 10.6 us  [ring_product(): held = lax.ppermute(held, axis, left)]
    dot_general x1 -> x4, matrix products: 5.06 us -> 5.89 us  [per_device(): jnp.einsum('sjnf,jfd->sjnd', part, lax.dynamic_slice_in_dim(w_down, start...]
  transfers between devices with their start and end apart: 4 -> 6, of which waited for: 4 -> 6; matrix products, arithmetic and copies ran while one was open for 3% -> 5% of each run, Pallas kernels for 0% -> 0%
where the time goes in v1:
time: 229 us; the launch traced here: 228 us
  waiting for transfers between devices  149 us (65%)
  blocking collectives  18.5 us (8%)
  matrix products  18.4 us (8%)
  starting transfers between devices  14.1 us (6%)
  between operations  13.6 us (6%)
  local copies, waits for them, and re-layouts  9.21 us (4%)
  other arithmetic  5.23 us (2%)
    reduce_scatter x1, waiting for transfers between devices, per_device(): lax.psum_scatter(up_part, 'tensor', scatter_dimension=3, tiled=True)  62.6 us
    reduce_scatter x1, waiting for transfers between devices, per_device(): lax.psum_scatter(gate_part, 'tensor', scatter_dimension=3, tiled=True)  54.5 us
    all_to_all x1, blocking collectives, per_device(): lax.all_to_all(outgoing, 'expert', split_axis=0, concat_axis=0, tiled=True)  18.5 us
    ppermute x3, waiting for transfers between devices, ring_product(): held = lax.ppermute(held, axis, left)  17.8 us
    all_to_all x1, waiting for transfers between devices, per_device(): lax.all_to_all(returned, 'expert', split_axis=0, concat_axis=0, tiled=True)  14.3 us
    ppermute x3, starting transfers between devices, ring_product(): held = lax.ppermute(held, axis, left)  10.6 us
    dot_general x1, matrix products, per_device(): jnp.einsum('sjnd,jdf->sjnf', received, w_up, preferred_element_type=jnp.f...  6.28 us
    dot_general x1, matrix products, per_device(): jnp.einsum('sjnd,jdf->sjnf', received, w_gate, preferred_element_type=jnp...  6.24 us
  transfers between devices with their start and end apart: 6, of which 6 were waited for; matrix products, arithmetic and copies ran while one was open for 5% of the time, Pallas kernels for 0%

profile of v1, /device:TPU:0, one launch (start us, length us, event | category | flops | bytes accessed | tf_op | source)
XLA Modules:
  0.0 228.3 jit_solution(15617010850192639946)
XLA Ops:
  6.5 0.0 copy-start
  6.5 0.0 reduce-scatter.3.cloned.1.call-start
  6.5 0.8 copy.16
  7.3 0.1 eq.33
  7.4 0.1 eq.29
  7.5 0.7 broadcast_multiply_fusion
  8.2 1.1 reduce-window.6
  9.4 0.2 slice_reduce_fusion
  9.6 0.1 copy.15
  9.7 0.1 mul.45
  9.8 0.1 fusion.28
  9.9 2.4 %scatter_custom_fusion = s32[512]{0:T(512)S(1)} fusion(s32[512]{0:T(512)S(1)} %bitcast.65, s32[512]{0:T(512)S(1)} %add_select_fusion, s32[]{:T(128)} %constant.57.clone.1), kind=kCustom, calls=%fused_computation.48 | custom fusion | bytes 2052 | tf_op jit(solution)/shard_map/scatter | solution.py:37
  12.4 0.1 broadcast_in_dim.26
  12.5 0.0 copy-done
  12.5 2.1 gather_fusion
  14.5 0.1 broadcast_select_fusion
  14.7 18.5 %all_to_all.10 = bf16[4,2,64,1024]{3,2,1,0:T(8,128)(2,1)S(1)} all-to-all(bf16[4,2,64,1024]{3,2,1,0:T(8,128)(2,1)S(1)} %broadcast_select_fusion), channel_id=1, replica_groups=mesh['group'=2,'expert'=4,'tensor'=4] {'expert'}, dimensions={0} | all-to-all | bytes 2097152 | tf_op jit(solution)/shard_map/all_to_all | solution.py:41
  33.2 6.2 %fusion.4 = f32[4,2,64,1536]{3,2,0,1:T(8,128)} fusion(bf16[2,1024,1536]{2,1,0:T(8,128)(2,1)} %param.7, bf16[4,2,64,1024]{3,2,1,0:T(8,128)(2,1)S(1)} %all_to_all.10), kind=kOutput, calls=%fused_computation.7 | convolution fusion | flops 1610612736 | bytes 10485760 | tf_op jit(solution)/shard_map/sjnd,jdf->sjnf/dot_general | solution.py:42
  39.4 0.0 reduce-scatter.3.cloned.1.call-update
  39.4 0.0 reduce-scatter.5.cloned.1.call-start
  39.5 6.3 %fusion.7 = f32[4,2,64,1536]{3,2,0,1:T(8,128)} fusion(bf16[2,1024,1536]{2,1,0:T(8,128)(2,1)} %param.8, bf16[4,2,64,1024]{3,2,1,0:T(8,128)(2,1)S(1)} %all_to_all.10), kind=kOutput, calls=%fused_computation.8 | convolution fusion | flops 1610612736 | bytes 10485760 | tf_op jit(solution)/shard_map/sjnd,jdf->sjnf/dot_general | solution.py:43
  45.8 0.0 reduce-scatter.5.cloned.1.call-update
  45.8 54.5 %reduce-scatter.3.cloned.1.call-done = f32[4,2,64,384]{3,2,0,1:T(8,128)} async-done(((f32[4,2,64,1536]{3,2,0,1:T(8,128)}), f32[4,2,64,384]{3,2,0,1:T(8,128)}) %reduce-scatter.3.cloned.1.call-update) | async-done | bytes 786448 | tf_op jit(solution)/shard_map/reduce_scatter | solution.py:44
  100.3 62.6 %reduce-scatter.5.cloned.1.call-done = f32[4,2,64,384]{3,2,0,1:T(8,128)} async-done(((f32[4,2,64,1536]{3,2,0,1:T(8,128)}), f32[4,2,64,384]{3,2,0,1:T(8,128)}) %reduce-scatter.5.cloned.1.call-update) | async-done | bytes 786448 | tf_op jit(solution)/shard_map/reduce_scatter | solution.py:45
  163.0 0.0 slice-start
  163.0 1.7 multiply_convert_fusion
  164.7 2.0 collective-permute-start
  166.7 8.5 %collective-permute-done = bf16[4,2,64,384]{3,2,0,1:T(8,128)(2,1)S(1)} collective-permute-done((bf16[4,2,64,384]{3,2,0,1:T(8,128)(2,1)S(1)}, bf16[4,2,64,384]{3,2,0,1:T(8,128)(2,1)S(1)}, u32[]{:S(2)}, u32[]{:S(2)}) %collective-permute-start) | collective-permute-done | bytes 393248 | tf_op jit(solution)/shard_map/ppermute | solution.py:14
  175.3 4.3 %collective-permute-start.1 = (bf16[4,2,64,384]{3,2,0,1:T(8,128)(2,1)S(1)}, bf16[4,2,64,384]{3,2,0,1:T(8,128)(2,1)S(1)}, u32[]{:S(2)}, u32[]{:S(2)}) collective-permute-start(bf16[4,2,64,384]{3,2,0,1:T(8,128)(2,1)S(1)} %collective-permute-done), channel_id=1, source_target_pairs={{0,3},{1,0},{2,1},{3,2},{4,7},{5,4},{6,5},{7,6},{8,11},{9,8},{10,9... | collective-permute-start | bytes 1179656 | tf_op jit(solution)/shard_map/ppermute | solution.py:14
  179.5 0.0 slice-start.1
  179.5 2.3 fusion.16
  181.8 5.4 %collective-permute-done.1 = bf16[4,2,64,384]{3,2,0,1:T(8,128)(2,1)S(1)} collective-permute-done((bf16[4,2,64,384]{3,2,0,1:T(8,128)(2,1)S(1)}, bf16[4,2,64,384]{3,2,0,1:T(8,128)(2,1)S(1)}, u32[]{:S(2)}, u32[]{:S(2)}) %collective-permute-start.1) | collective-permute-done | bytes 393248 | tf_op jit(solution)/shard_map/ppermute | solution.py:14
  187.2 4.3 %collective-permute-start.2 = (bf16[4,2,64,384]{3,2,0,1:T(8,128)(2,1)S(1)}, bf16[4,2,64,384]{3,2,0,1:T(8,128)(2,1)S(1)}, u32[]{:S(2)}, u32[]{:S(2)}) collective-permute-start(bf16[4,2,64,384]{3,2,0,1:T(8,128)(2,1)S(1)} %collective-permute-done.1), channel_id=1, source_target_pairs={{0,3},{1,0},{2,1},{3,2},{4,7},{5,4},{6,5},{7,6},{8,11},{9,8},{10,9... | collective-permute-start | bytes 1179656 | tf_op jit(solution)/shard_map/ppermute | solution.py:14
  191.5 2.1 fusion.14
  193.6 0.0 slice-done
  193.6 0.0 slice-done.1
  193.6 0.7 fusion.12
  194.4 3.9 %collective-permute-done.2 = bf16[4,2,64,384]{3,2,0,1:T(8,128)(2,1)S(1)} collective-permute-done((bf16[4,2,64,384]{3,2,0,1:T(8,128)(2,1)S(1)}, bf16[4,2,64,384]{3,2,0,1:T(8,128)(2,1)S(1)}, u32[]{:S(2)}, u32[]{:S(2)}) %collective-permute-start.2) | collective-permute-done | bytes 393248 | tf_op jit(solution)/shard_map/ppermute | solution.py:14
  198.3 0.8 fusion.22
  199.1 0.0 copy-start.1
  199.1 1.1 copy.20
  200.2 3.5 %all-to-all-start.1 = ((bf16[4,2,64,1024]{3,2,1,0:T(8,128)(2,1)}), bf16[4,2,64,1024]{3,2,1,0:T(8,128)(2,1)S(1)}, u32[]{:S(2)}, u32[]{:S(2)}) async-start(bf16[4,2,64,1024]{3,2,1,0:T(8,128)(2,1)} %copy.20), calls=%async_computation.3 | async-start | bytes 2097152 | tf_op jit(solution)/shard_map/all_to_all | solution.py:59
  203.7 0.0 copy-done.1
  203.7 0.1 copy.21
  203.8 14.3 %all-to-all-done.1 = bf16[4,2,64,1024]{3,2,1,0:T(8,128)(2,1)S(1)} async-done(((bf16[4,2,64,1024]{3,2,1,0:T(8,128)(2,1)}), bf16[4,2,64,1024]{3,2,1,0:T(8,128)(2,1)S(1)}, u32[]{:S(2)}, u32[]{:S(2)}) %all-to-all-start.1) | async-done | bytes 1048608 | tf_op jit(solution)/shard_map/all_to_all | solution.py:59
  218.1 2.0 gather_fusion.1
  220.2 1.3 fusion.10
  (10 shorter events, 0.1 us)
Async XLA Ops:
  6.5 6.0 %copy-start = (bf16[64,1024]{1,0:T(8,128)(2,1)S(1)}, bf16[64,1024]{1,0:T(8,128)(2,1)}, u32[]{:S(2)}) copy-start(bf16[64,1024]{1,0:T(8,128)(2,1)} %param.6) | copy-start | bytes 393220
  6.5 93.8 %reduce-scatter.3.cloned.1.call-start = ((), (), s32[]{:S(2)}) async-start(), calls=%async_computation.4 | async-start | bytes 3932160 | tf_op jit(solution)/shard_map/reduce_scatter | solution.py:44
  39.4 123.5 %reduce-scatter.5.cloned.1.call-start = ((), (), s32[]{:S(2)}) async-start(), calls=%async_computation.5 | async-start | bytes 3932160 | tf_op jit(solution)/shard_map/reduce_scatter | solution.py:45
  163.0 30.6 %slice-start = ((s8[6291456]{0:T(1024)(128)(4,1)}), s8[2097152]{0:T(1024)(128)(4,1)S(1)}, s32[]{:S(2)}) async-start(s8[6291456]{0:T(1024)(128)(4,1)} %bitcast.62), calls=%async_computation.6 | async-start | bytes 4194304
  164.7 10.5 %collective-permute-start = (bf16[4,2,64,384]{3,2,0,1:T(8,128)(2,1)S(1)}, bf16[4,2,64,384]{3,2,0,1:T(8,128)(2,1)S(1)}, u32[]{:S(2)}, u32[]{:S(2)}) collective-permute-start(bf16[4,2,64,384]{3,2,0,1:T(8,128)(2,1)S(1)} %multiply_convert_fusion), channel_id=1, source_target_pairs={{0,3},{1,0},{2,1},{3,2},{4,7},{5,4},{6,5},{7,6},{8,11},{9,8},{10,9... | collective-permute-start | bytes 1179656 | tf_op jit(solution)/shard_map/ppermute | solution.py:14
  175.3 11.9 %collective-permute-start.1 = (bf16[4,2,64,384]{3,2,0,1:T(8,128)(2,1)S(1)}, bf16[4,2,64,384]{3,2,0,1:T(8,128)(2,1)S(1)}, u32[]{:S(2)}, u32[]{:S(2)}) collective-permute-start(bf16[4,2,64,384]{3,2,0,1:T(8,128)(2,1)S(1)} %collective-permute-done), channel_id=1, source_target_pairs={{0,3},{1,0},{2,1},{3,2},{4,7},{5,4},{6,5},{7,6},{8,11},{9,8},{10,9... | collective-permute-start | bytes 1179656 | tf_op jit(solution)/shard_map/ppermute | solution.py:14
  179.5 14.1 %slice-start.1 = ((s8[6291456]{0:T(1024)(128)(4,1)}), s8[4194304]{0:T(1024)(128)(4,1)S(1)}, s32[]{:S(2)}) async-start(s8[6291456]{0:T(1024)(128)(4,1)} %bitcast.62), calls=%async_computation.7 | async-start | bytes 8388608
  187.2 11.1 %collective-permute-start.2 = (bf16[4,2,64,384]{3,2,0,1:T(8,128)(2,1)S(1)}, bf16[4,2,64,384]{3,2,0,1:T(8,128)(2,1)S(1)}, u32[]{:S(2)}, u32[]{:S(2)}) collective-permute-start(bf16[4,2,64,384]{3,2,0,1:T(8,128)(2,1)S(1)} %collective-permute-done.1), channel_id=1, source_target_pairs={{0,3},{1,0},{2,1},{3,2},{4,7},{5,4},{6,5},{7,6},{8,11},{9,8},{10,9... | collective-permute-start | bytes 1179656 | tf_op jit(solution)/shard_map/ppermute | solution.py:14
  199.1 4.6 %copy-start.1 = (f32[64,8]{0,1:T(8,128)S(1)}, f32[64,8]{0,1:T(8,128)}, u32[]{:S(2)}) copy-start(f32[64,8]{0,1:T(8,128)} %param.11) | copy-start | bytes 6148
  200.2 17.9 %all-to-all-start.1 = ((bf16[4,2,64,1024]{3,2,1,0:T(8,128)(2,1)}), bf16[4,2,64,1024]{3,2,1,0:T(8,128)(2,1)S(1)}, u32[]{:S(2)}, u32[]{:S(2)}) async-start(bf16[4,2,64,1024]{3,2,1,0:T(8,128)(2,1)} %copy.20), calls=%async_computation.3 | async-start | bytes 2097152 | tf_op jit(solution)/shard_map/all_to_all | solution.py:59
Sparse Core Ops, SparseCore 0:
  39.6 60.7 reduce-scatter.2
  102.6 60.3 reduce-scatter.4
